TPU v7x, 32 devices: a whole 2x2x4 slice. The times are simulated.
32 devices in a mesh: dp: 8 (over z, core), row: 2 (over x), col: 2 (over y).
Axes of the slice: x: 2, y: 2, z: 4, core: 2. Of those that a mesh axis runs over, the one named last changes fastest.
Arguments:
- tokens: bfloat16 [4096, 8192], P(('dp', 'row', 'col')), parts along dimension 0, may hold values from -6 to 6
- w_gate: bfloat16 [8192, 1024], P(('row', 'col')), may hold values from -0.0625 to 0.0625
- w_up: bfloat16 [8192, 1024], P(('row', 'col')), may hold values from -0.0625 to 0.0625
- w_down: bfloat16 [1024, 8192], P(None, ('row', 'col')), may hold values from -0.1875 to 0.1875
Outputs:
- mixed: bfloat16 [4096, 8192], P(('dp', 'row', 'col')), parts along dimension 0
There are 8 independent parts, one for each index of `dp`. A program takes and returns all parts, laid end to end along the dimension named above; an argument that names none is the same for every part. Nothing has to cross between parts.
All inputs are finite; a program needn't handle non-finite values.
Results may differ from a plain program's by a relative error of at most 0.029.
Values may be sent and summed in bfloat16 or wider, within the bound.
A program may use at most 64 MiB of HBM per device.

v0:
```python
import jax
import jax.numpy as jnp
from jax import lax
from jax.sharding import PartitionSpec as P


def swiglu(sums, hidden_width):
    return (jax.nn.silu(sums[:, :hidden_width]) * sums[:, hidden_width:]).astype(jnp.bfloat16)


def shards(tokens, w_gate, w_up, w_down):
    hidden_width = w_gate.shape[1]
    col_tokens = lax.all_to_all(tokens, "row", split_axis=1, concat_axis=0, tiled=True)
    gate_rows, up_rows = (
        lax.all_gather(w_gate, "col", axis=0, tiled=True),
        lax.all_gather(w_up, "col", axis=0, tiled=True),
    )
    paired = jnp.concatenate([gate_rows, up_rows], axis=1)
    own_hidden = swiglu(
        lax.psum_scatter(
            jnp.dot(col_tokens, paired, preferred_element_type=jnp.float32).astype(jnp.bfloat16),
            "row",
            scatter_dimension=0,
            tiled=True,
        ).astype(jnp.float32),
        hidden_width,
    )
    out_whole = jnp.dot(
        lax.all_gather(own_hidden, ("row", "col"), axis=0, tiled=True),
        w_down,
        preferred_element_type=jnp.float32,
    )
    out_ready = out_whole.astype(jnp.bfloat16)
    return lax.all_to_all(out_ready, ("row", "col"), split_axis=0, concat_axis=1, tiled=True)


def solution(mesh):
    in_specs = (
        P(("dp", "row", "col"), None),
        P(("row", "col"), None),
        P(("row", "col"), None),
        P(None, ("row", "col")),
    )
    out_specs = P(("dp", "row", "col"), None)
    return jax.shard_map(shards, mesh=mesh, in_specs=in_specs, out_specs=out_specs, check_vma=False)
```

profile of v0, /device:TPU:0, one launch (start us, length us, event | category | flops | bytes accessed | tf_op | source)
XLA Modules:
  0.0 324.1 jit_solution(12852378790055556145)
XLA Ops:
  6.5 0.0 all-gather.4.cloned.1.call-start
  6.5 0.7 all-gather.4.cloned.1.call-update
  7.3 0.0 all-gather.6.cloned.1.call-start
  7.3 0.7 all-gather.6.cloned.1.call-update
  8.0 0.0 reduce-scatter.4.cloned.1.call-start
  8.1 0.1 copy-done
  8.1 2.4 copy.10
  10.5 30.1 %all_to_all.38 = bf16[128,2,4096]{0,2,1:T(8,128)(2,1)S(1)} all-to-all(bf16[128,2,4096]{0,2,1:T(8,128)(2,1)} %bitcast.15), channel_id=1, replica_groups=mesh['dp'=8,'row'=2,'col'=2] {'row'}, dimensions={1} | all-to-all | bytes 4194304 | tf_op jit(solution)/shard_map/all_to_all | solution.py:13
  40.6 2.7 copy.11
  43.3 72.3 %all-gather.4.cloned.1.call-done = bf16[4096,1024]{1,0:T(8,128)(2,1)} async-done(((bf16[2048,1024]{1,0:T(8,128)(2,1)}), bf16[4096,1024]{1,0:T(8,128)(2,1)}) %all-gather.4.cloned.1.call-update) | async-done | bytes 8388624 | tf_op jit(solution)/shard_map/all_gather | solution.py:15
  115.6 105.6 %all-gather.6.cloned.1.call-done = bf16[4096,1024]{1,0:T(8,128)(2,1)} async-done(((bf16[2048,1024]{1,0:T(8,128)(2,1)}), bf16[4096,1024]{1,0:T(8,128)(2,1)}) %all-gather.6.cloned.1.call-update) | async-done | bytes 8388624 | tf_op jit(solution)/shard_map/all_gather | solution.py:16
  221.2 11.3 %fusion.7 = bf16[256,2048]{0,1:T(8,128)(2,1)S(1)} fusion(bf16[256,4096]{1,0:T(8,128)(2,1)} %bitcast.16, bf16[4096,1024]{1,0:T(8,128)(2,1)} %all-gather.6.cloned.1.call-done, bf16[4096,1024]{1,0:T(8,128)(2,1)} %all-gather.4.cloned.1.call-done), kind=kOutput, calls=%fused_computation.6 | convolution fusion | flops 4329046016 | bytes 19922944 | tf_op jit(solution)/shard_map/dot_general | solution.py:21
  232.5 1.4 copy.13
  233.9 0.0 reduce-scatter.4.cloned.1.call-update
  233.9 0.0 all-gather.8.cloned.1.call-start
  234.0 20.5 %reduce-scatter.4.cloned.1.call-done = bf16[128,2048]{1,0:T(8,128)(2,1)} async-done(((bf16[256,2048]{1,0:T(8,128)(2,1)}), bf16[128,2048]{1,0:T(8,128)(2,1)}) %reduce-scatter.4.cloned.1.call-update) | async-done | bytes 524304
  254.5 1.3 copy.14
  255.8 0.1 convert_element_type.17
  255.9 0.8 fusion.10
  256.7 0.0 all-gather.8.cloned.1.call-update
  256.7 26.5 %all-gather.8.cloned.1.call-done = bf16[512,1024]{0,1:T(8,128)(2,1)} async-done(((bf16[128,1024]{0,1:T(8,128)(2,1)}), bf16[512,1024]{0,1:T(8,128)(2,1)}) %all-gather.8.cloned.1.call-update) | async-done | bytes 1048592 | tf_op jit(solution)/shard_map/all_gather | solution.py:29
  283.3 4.9 %convolution_convert_fusion = bf16[512,2048]{1,0:T(8,128)(2,1)S(1)} fusion(bf16[512,1024]{0,1:T(8,128)(2,1)} %all-gather.8.cloned.1.call-done, bf16[1024,2048]{1,0:T(8,128)(2,1)} %param.7), kind=kOutput, calls=%fused_computation.4 | convolution fusion | flops 2148532224 | bytes 7340032 | tf_op jit(solution)/shard_map/dot_general | solution.py:28
  288.2 28.0 %all_to_all.39 = bf16[4,128,2048]{2,1,0:T(8,128)(2,1)S(1)} all-to-all(bf16[4,128,2048]{2,1,0:T(8,128)(2,1)S(1)} %bitcast.17), channel_id=1, replica_groups=mesh['dp'=8,'row'=2,'col'=2] {'row','col'}, dimensions={0} | all-to-all | bytes 4194304 | tf_op jit(solution)/shard_map/all_to_all | solution.py:34
  316.1 1.5 copy.15
  (1 shorter events, 0.0 us)
Async XLA Ops:
  6.5 1.6 copy-start
  6.5 109.1 %all-gather.4.cloned.1.call-start = ((), (), s32[]{:S(2)}) async-start(), calls=%async_computation.3 | async-start | bytes 12582912 | tf_op jit(solution)/shard_map/all_gather | solution.py:15
  7.3 213.9 %all-gather.6.cloned.1.call-start = ((), (), s32[]{:S(2)}) async-start(), calls=%async_computation.4 | async-start | bytes 12582912 | tf_op jit(solution)/shard_map/all_gather | solution.py:16
  8.0 246.5 %reduce-scatter.4.cloned.1.call-start = ((), (), s32[]{:S(2)}) async-start(), calls=%async_computation.6 | async-start | bytes 1572864
  233.9 49.3 %all-gather.8.cloned.1.call-start = ((), (), s32[]{:S(2)}) async-start(), calls=%async_computation.5 | async-start | bytes 1310720 | tf_op jit(solution)/shard_map/all_gather | solution.py:29
Sparse Core Ops, SparseCore 0:
  8.9 106.6 all-gather.3
  117.2 103.9 all-gather.5
  234.1 20.3 reduce-scatter.3
  256.9 26.3 all-gather.7
where the time goes:
time: 324 us
  waiting for transfers between devices  226 us (70%)
  blocking collectives  58 us (18%)
  matrix products  16.2 us (5%)
  between operations  13.2 us (4%)
  local copies, waits for them, and re-layouts  9.38 us (3%)
    all_gather x1, waiting for transfers between devices, shards(): lax.all_gather(w_up, 'col', axis=0, tiled=True)  106 us
    all_gather x1, waiting for transfers between devices, shards(): lax.all_gather(w_gate, 'col', axis=0, tiled=True)  72.3 us
    all_to_all x1, blocking collectives, shards(): lax.all_to_all(tokens, 'row', split_axis=1, concat_axis=0, tiled=True)  30.1 us
    all_to_all x1, blocking collectives, shards(): lax.all_to_all(out_ready, ('row', 'col'), split_axis=0, concat_axis=1, ti...  28 us
    all_gather x1, waiting for transfers between devices, shards(): lax.all_gather(own_hidden, ('row', 'col'), axis=0, tiled=True)  26.5 us
    unnamed x5, waiting for transfers between devices  21.9 us
    dot_general x1, matrix products, shards(): jnp.dot(col_tokens, paired, preferred_element_type=jnp.float32)  11.3 us
  transfers between devices with their start and end apart: 4, of which 4 were waited for; matrix products, arithmetic and copies ran while one was open for 2% of the time, Pallas kernels for 0%

commit v1 on v0

v1 whole, which is shorter than its diff:
```python
import functools

import jax
import jax.numpy as jnp
from jax import lax
from jax.experimental import pallas as pl
from jax.experimental.pallas import tpu as pltpu
from jax.sharding import PartitionSpec as P

MESH = pl.DeviceIdType.MESH
CHUNKS = 2


def tile_of(width, most):
    tile = min(width, most)
    while width % tile:
        tile //= 2
    return tile


def kernel(
    rows, cols, chunks,
    x_ref, wg_ref, wu_ref, wd_ref, out_ref,
    wg, wu, wd, xbuf, acc, psend, prec, hbuf, osend,
    w_sem, x_send, x_recv, p_send, p_recv, h_send, h_recv, o_send, o_recv,
):
    n = rows * cols
    row, col = lax.axis_index("row"), lax.axis_index("col")
    me = row * cols + col
    tokens = x_ref.shape[0]
    t = tokens // chunks
    features = wg.shape[0]
    hidden = wg.shape[1]
    out_cols = wd.shape[1]
    bf16, f32 = jnp.bfloat16, jnp.float32

    def worker(o):
        r = lax.rem(row + o // cols, rows)
        c = lax.rem(col + lax.rem(o, cols), cols)
        return r, c

    def owner(o):
        r = lax.rem(row - o // cols + rows, rows)
        c = lax.rem(col - lax.rem(o, cols) + cols, cols)
        return r, c

    def at(rc):
        return {"row": rc[0], "col": rc[1]}

    def x_copy(c, o):
        r_, c_ = worker(o)
        start = pl.multiple_of((r_ * cols + c_) * features, features)
        return pltpu.make_async_remote_copy(
            src_ref=x_ref.at[pl.ds(c * t, t), pl.ds(start, features)],
            dst_ref=xbuf.at[c, o],
            send_sem=x_send.at[c, o], recv_sem=x_recv.at[c, o],
            device_id=at((r_, c_)), device_id_type=MESH,
        )

    def x_own(c):
        start = pl.multiple_of(me * features, features)
        return pltpu.make_async_copy(
            x_ref.at[pl.ds(c * t, t), pl.ds(start, features)], xbuf.at[c, 0], x_recv.at[c, 0]
        )

    def p_copy(c, o):
        return pltpu.make_async_remote_copy(
            src_ref=psend.at[c, o], dst_ref=prec.at[c, o],
            send_sem=p_send.at[c, o], recv_sem=p_recv.at[c, o],
            device_id=at(owner(o)), device_id_type=MESH,
        )

    def h_copy(c, o):
        return pltpu.make_async_remote_copy(
            src_ref=hbuf.at[c, 0], dst_ref=hbuf.at[c, o],
            send_sem=h_send.at[c, o], recv_sem=h_recv.at[c, o],
            device_id=at(worker(o)), device_id_type=MESH,
        )

    def o_copy(c, o):
        start = pl.multiple_of(me * out_cols, out_cols)
        return pltpu.make_async_remote_copy(
            src_ref=osend.at[c, o],
            dst_ref=out_ref.at[pl.ds(c * t, t), pl.ds(start, out_cols)],
            send_sem=o_send.at[c, o], recv_sem=o_recv.at[c, o],
            device_id=at(owner(o)), device_id_type=MESH,
        )

    def o_arrival(c, o):
        r_, c_ = worker(o)
        start = pl.multiple_of((r_ * cols + c_) * out_cols, out_cols)
        return pltpu.make_async_remote_copy(
            src_ref=osend.at[c, o],
            dst_ref=out_ref.at[pl.ds(c * t, t), pl.ds(start, out_cols)],
            send_sem=o_send.at[c, o], recv_sem=o_recv.at[c, o],
            device_id=at(owner(o)), device_id_type=MESH,
        )

    def o_own(c):
        start = pl.multiple_of(me * out_cols, out_cols)
        return pltpu.make_async_copy(
            osend.at[c, 0], out_ref.at[pl.ds(c * t, t), pl.ds(start, out_cols)], o_recv.at[c, 0]
        )

    loads = [
        pltpu.make_async_copy(wg_ref, wg, w_sem.at[0]),
        pltpu.make_async_copy(wu_ref, wu, w_sem.at[1]),
        pltpu.make_async_copy(wd_ref, wd, w_sem.at[2]),
    ]

    barrier = pltpu.get_barrier_semaphore()
    for o in range(1, n):
        pl.semaphore_signal(barrier, inc=1, device_id=at(worker(o)), device_id_type=MESH)
    pl.semaphore_wait(barrier, n - 1)

    for c in range(chunks):
        for o in range(1, n):
            x_copy(c, o).start()
    for c in range(chunks):
        x_own(c).start()
    for load in loads:
        load.start()
    loads[0].wait()
    loads[1].wait()

    up_tile = tile_of(hidden, 512)

    def first(i, _):
        c, o = i // n, lax.rem(i, n)

        @pl.when(o == 0)
        def _():
            x_own(c).wait()

        @pl.when(o != 0)
        def _():
            x_copy(c, o).wait_recv()

        def tile(j, _):
            at_gate = pl.multiple_of(j * up_tile, up_tile)
            at_up = pl.multiple_of(hidden + j * up_tile, up_tile)
            gate = jnp.dot(xbuf[c, o], wg[:, pl.ds(at_gate, up_tile)], preferred_element_type=f32)
            up = jnp.dot(xbuf[c, o], wu[:, pl.ds(at_gate, up_tile)], preferred_element_type=f32)

            @pl.when(o == 0)
            def _():
                acc[c, :, pl.ds(at_gate, up_tile)] = gate
                acc[c, :, pl.ds(at_up, up_tile)] = up

            @pl.when(o != 0)
            def _():
                psend[c, o, :, pl.ds(at_gate, up_tile)] = gate.astype(bf16)
                psend[c, o, :, pl.ds(at_up, up_tile)] = up.astype(bf16)

            return 0

        lax.fori_loop(0, hidden // up_tile, tile, 0)

        @pl.when(o != 0)
        def _():
            p_copy(c, o).start()

        return 0

    lax.fori_loop(0, n * chunks, first, 0)

    sub = tile_of(t, 16)

    def second(c, _):
        def arrive(o, _):
            p_copy(c, o).wait_recv()
            return 0

        lax.fori_loop(1, n, arrive, 0)

        def block(b, _):
            at_row = pl.ds(pl.multiple_of(b * sub, sub), sub)
            gate = acc[c, at_row, pl.ds(0, hidden)]
            up = acc[c, at_row, pl.ds(hidden, hidden)]
            for o in range(1, n):
                gate = gate + prec[c, o, at_row, pl.ds(0, hidden)].astype(f32)
                up = up + prec[c, o, at_row, pl.ds(hidden, hidden)].astype(f32)
            hbuf[c, 0, at_row, :] = (gate / (1.0 + jnp.exp(-gate)) * up).astype(bf16)
            return 0

        lax.fori_loop(0, t // sub, block, 0)
        for o in range(1, n):
            h_copy(c, o).start()
        return 0

    lax.fori_loop(0, chunks, second, 0)

    loads[2].wait()
    down_tile = tile_of(out_cols, 512)

    def third(i, _):
        c, o = i // n, lax.rem(i, n)

        @pl.when(o != 0)
        def _():
            h_copy(c, o).wait_recv()

        def tile(j, _):
            where = pl.ds(pl.multiple_of(j * down_tile, down_tile), down_tile)
            osend[c, o, :, where] = jnp.dot(
                hbuf[c, o], wd[:, where], preferred_element_type=f32
            ).astype(bf16)
            return 0

        lax.fori_loop(0, out_cols // down_tile, tile, 0)

        @pl.when(o == 0)
        def _():
            o_own(c).start()

        @pl.when(o != 0)
        def _():
            o_copy(c, o).start()

        return 0

    lax.fori_loop(0, n * chunks, third, 0)

    for c in range(chunks):
        o_own(c).wait()
        for o in range(1, n):
            x_copy(c, o).wait_send()
            p_copy(c, o).wait_send()
            h_copy(c, o).wait_send()
            o_copy(c, o).wait_send()
            o_arrival(c, o).wait_recv()


def solution(mesh):
    rows, cols = mesh.shape["row"], mesh.shape["col"]
    n = rows * cols

    def shards(tokens, w_gate, w_up, w_down):
        count, width = tokens.shape
        features, hidden = w_gate.shape
        out_cols = w_down.shape[1]
        chunks = CHUNKS
        t = count // chunks
        bf16 = jnp.bfloat16
        pair = pltpu.SemaphoreType.DMA((chunks, n))
        any_space = pl.BlockSpec(memory_space=pl.ANY)
        return pl.pallas_call(
            functools.partial(kernel, rows, cols, chunks),
            out_shape=jax.ShapeDtypeStruct((count, width), bf16),
            in_specs=[any_space] * 4,
            out_specs=any_space,
            scratch_shapes=[
                pltpu.VMEM((features, hidden), bf16),
                pltpu.VMEM((features, hidden), bf16),
                pltpu.VMEM((hidden, out_cols), bf16),
                pltpu.VMEM((chunks, n, t, features), bf16),
                pltpu.VMEM((chunks, t, 2 * hidden), jnp.float32),
                pltpu.VMEM((chunks, n, t, 2 * hidden), bf16),
                pltpu.VMEM((chunks, n, t, 2 * hidden), bf16),
                pltpu.VMEM((chunks, n, t, hidden), bf16),
                pltpu.VMEM((chunks, n, t, out_cols), bf16),
                pltpu.SemaphoreType.DMA((3,)),
                pair, pair, pair, pair, pair, pair, pair, pair,
            ],
            compiler_params=pltpu.CompilerParams(collective_id=0, has_side_effects=True),
        )(tokens, w_gate, w_up, w_down)

    in_specs = (
        P(("dp", "row", "col"), None),
        P(("row", "col"), None),
        P(("row", "col"), None),
        P(None, ("row", "col")),
    )
    out_specs = P(("dp", "row", "col"), None)
    return jax.shard_map(shards, mesh=mesh, in_specs=in_specs, out_specs=out_specs, check_vma=False)
```

time: 324 us -> 87.9 us (0.27)
  waiting for transfers between devices: 226 us -> 0 us
  Pallas kernels: 0 us -> 84.6 us
  blocking collectives: 58 us -> 0 us
  matrix products: 16.2 us -> 0 us
  between operations: 13.2 us -> 0.01 us
  local copies, waits for them, and re-layouts: 9.38 us -> 3.1 us
    all_gather x3 -> x0, waiting for transfers between devices: 204 us -> none  [the longest x1 106 us: shards(): lax.all_gather(w_up, 'col', axis=0, tiled=True)]
    pallas_call x0 -> x1, Pallas kernels: none -> 84.6 us  [shards(): pl.pallas_call(functools.partial(kernel, rows, cols, chunks), out_shape=j...]
    all_to_all x2 -> x0, blocking collectives: 58 us -> none  [the longest x1 30.1 us: shards(): lax.all_to_all(tokens, 'row', split_axis=1, concat_axis=0, tiled=True)]
    unnamed x5 -> x0, waiting for transfers between devices: 21.9 us -> none
    dot_general x2 -> x0, matrix products: 16.2 us -> none  [the longest x1 11.3 us: shards(): jnp.dot(col_tokens, paired, preferred_element_type=jnp.float32)]
    all_to_all x2 -> x0, local copies, waits for them, and re-layouts: 4.16 us -> none  [the longest x1 2.71 us: shards(): lax.all_to_all(tokens, 'row', split_axis=1, concat_axis=0, tiled=True)]
  transfers between devices with their start and end apart: 4 -> 0, of which waited for: 4 -> 0; matrix products, arithmetic and copies ran while one was open for 2% -> 0% of each run, Pallas kernels for 0% -> 0%
where the time goes in v1:
time: 87.9 us; the launch traced here: 87.7 us
  Pallas kernels  84.6 us (96%)
  local copies, waits for them, and re-layouts  3.1 us (4%)
    pallas_call x1, Pallas kernels, shards(): pl.pallas_call(functools.partial(kernel, rows, cols, chunks), out_shape=j...  84.6 us
    unnamed x1, local copies, waits for them, and re-layouts  3.1 us

profile of v1, /device:TPU:0, one launch (start us, length us, event | category | flops | bytes accessed | tf_op | source)
XLA Modules:
  0.0 87.7 jit_solution(2911146566784884263)
XLA Ops:
  0.0 84.6 %shard_map.46 = bf16[128,8192]{1,0:T(8,128)(2,1)} custom-call(bf16[128,8192]{1,0:T(8,128)(2,1)} %x_ref.1, bf16[2048,1024]{1,0:T(8,128)(2,1)} %wg_ref.1, bf16[2048,1024]{1,0:T(8,128)(2,1)} %wu_ref.1, bf16[1024,2048]{1,0:T(8,128)(2,1)} %wd_ref.1), custom_call_target="tpu_custom_call" | custom-call | tf_op jit(solution)/shard_map/pallas_call | solution.py:247
  84.7 3.1 %copy.6 = bf16[128,8192]{1,0:T(8,128)(2,1)} copy(bf16[128,8192]{1,0:T(8,128)(2,1)} %shard_map.46) | data formatting | bytes 4194304

commit v2 on v0

v2 whole, which is shorter than its diff:
```python
import functools

import jax
import jax.numpy as jnp
from jax import lax
from jax.experimental import pallas as pl
from jax.experimental.pallas import tpu as pltpu
from jax.sharding import PartitionSpec as P

MESH = pl.DeviceIdType.MESH
CHUNKS = 4
AHEAD = 2


def tile_of(width, most):
    tile = min(width, most)
    while width % tile:
        tile //= 2
    return tile


def kernel(
    rows, cols, chunks,
    x_ref, wg_ref, wu_ref, wd_ref, out_ref,
    wg, wu, wd, xbuf, acc, part, rec_a, rec_b, sum_a, sum_b, fin_a, fin_b, hbuf, osend,
    w_sem, x_sem, a_sem, b_sem, c_sem, d_sem, h_sem, ra_sem, rb_sem, o_sem,
):
    n = rows * cols
    row, col = lax.axis_index("row"), lax.axis_index("col")
    me = row * cols + col
    t = x_ref.shape[0] // chunks
    features, hidden = wg.shape
    half = hidden // 2
    out_cols = wd.shape[1]
    bf16, f32 = jnp.bfloat16, jnp.float32

    def up(r, c):
        return lax.rem(row + r, rows), lax.rem(col + c, cols)

    def down(r, c):
        return lax.rem(row + rows - r, rows), lax.rem(col + cols - c, cols)

    def shard(rc, width):
        return pl.ds(pl.multiple_of((rc[0] * cols + rc[1]) * width, width), width)

    def remote(src, dst, sems, index, to):
        return pltpu.make_async_remote_copy(
            src_ref=src, dst_ref=dst,
            send_sem=sems.at[(0, *index)], recv_sem=sems.at[(1, *index)],
            device_id={"row": to[0], "col": to[1]}, device_id_type=MESH,
        )

    def tok(k):
        return pl.ds(pl.multiple_of(k * t, t), t)

    slots = [(r, c) for r in range(rows) for c in range(cols)]
    others = slots[1:]

    def at_slot(r, c):
        return pl.ds((r * cols + c) * t, t)

    def x_copy(k, r, c):
        to = up(r, c)
        return remote(
            x_ref.at[tok(k), shard(to, features)], xbuf.at[k, at_slot(r, c)],
            x_sem, (k, r * cols + c), to,
        )

    def x_own(k):
        return pltpu.make_async_copy(
            x_ref.at[tok(k), shard((row, col), features)], xbuf.at[k, at_slot(0, 0)], x_sem.at[1, k, 0]
        )

    def a_copy(k, r):
        return remote(part.at[k, 0, r], rec_a.at[k, r], a_sem, (k, r), down(r, 0))

    def b_copy(k, c):
        return remote(part.at[k, 1, :, c], rec_b.at[k, c], b_sem, (k, c), down(0, c))

    def c_copy(k, c):
        return remote(sum_a.at[k, c], fin_a.at[k, c], c_sem, (k, c), down(0, c))

    def d_copy(k, r):
        return remote(sum_b.at[k, r], fin_b.at[k, r], d_sem, (k, r), down(r, 0))

    def h_copy(k, r, c):
        return remote(
            hbuf.at[k, at_slot(0, 0)], hbuf.at[k, at_slot(r, c)], h_sem, (k, r * cols + c), up(r, c)
        )

    def relay_a(k, r, c):
        return remote(
            hbuf.at[k, at_slot(r, 0), pl.ds(0, half)], hbuf.at[k, at_slot(r, c), pl.ds(0, half)],
            ra_sem, (k, r * cols + c), up(0, c),
        )

    def relay_b(k, r, c):
        return remote(
            hbuf.at[k, at_slot(0, c), pl.ds(half, half)], hbuf.at[k, at_slot(r, c), pl.ds(half, half)],
            rb_sem, (k, r * cols + c), up(r, 0),
        )

    def o_copy(k, r, c, columns_of):
        return remote(
            osend.at[k, at_slot(r, c)], out_ref.at[tok(k), shard(columns_of, out_cols)],
            o_sem, (k, r * cols + c), down(r, c),
        )

    def o_own(k):
        return pltpu.make_async_copy(
            osend.at[k, at_slot(0, 0)], out_ref.at[tok(k), shard((row, col), out_cols)], o_sem.at[1, k, 0]
        )

    edges = [(r, c) for r, c in others if r == 0 or c == 0]
    corners = [(r, c) for r, c in others if r and c]

    loads = [
        pltpu.make_async_copy(wg_ref, wg, w_sem.at[0]),
        pltpu.make_async_copy(wu_ref, wu, w_sem.at[1]),
        pltpu.make_async_copy(wd_ref, wd, w_sem.at[2]),
    ]

    barrier = pltpu.get_barrier_semaphore()
    for r, c in others:
        to = up(r, c)
        pl.semaphore_signal(barrier, inc=1, device_id={"row": to[0], "col": to[1]}, device_id_type=MESH)
    pl.semaphore_wait(barrier, n - 1)

    def send_tokens(k):
        for r, c in others:
            x_copy(k, r, c).start()

    for k in range(min(AHEAD, chunks)):
        send_tokens(k)
    for k in range(chunks):
        x_own(k).start()
    for load in loads:
        load.start()
    loads[0].wait()
    loads[1].wait()

    tile = tile_of(half, 512)
    per_half = half // tile

    def project(k):
        x_own(k).wait()
        for r, c in others:
            x_copy(k, r, c).wait_recv()

        def column(j, _):
            side, at = j // per_half, lax.rem(j, per_half) * tile
            source = pl.ds(pl.multiple_of(j * tile, tile), tile)
            for w, base in ((wg, 0), (wu, half)):
                target = pl.ds(pl.multiple_of(base + at, tile), tile)
                got = jnp.dot(xbuf[k], w[:, source], preferred_element_type=f32)
                acc[k, side, :, target] = got[:t]
                for r, c in others:
                    first = (r * cols + c) * t
                    part[k, side, r, c, :, target] = got[first : first + t].astype(bf16)
            return 0

        lax.fori_loop(0, 2 * per_half, column, 0)
        for r in range(1, rows):
            a_copy(k, r).start()
        for c in range(1, cols):
            b_copy(k, c).start()

    def combine(k):
        for r in range(1, rows):
            a_copy(k, r).wait_recv()
        for c in range(1, cols):
            total = part[k, 0, 0, c].astype(f32)
            for r in range(1, rows):
                total = total + rec_a[k, r, c].astype(f32)
            sum_a[k, c] = total.astype(bf16)
            c_copy(k, c).start()
        for c in range(1, cols):
            b_copy(k, c).wait_recv()
        for r in range(1, rows):
            total = part[k, 1, r, 0].astype(f32)
            for c in range(1, cols):
                total = total + rec_b[k, c, r].astype(f32)
            sum_b[k, r] = total.astype(bf16)
            d_copy(k, r).start()

    def activate(k):
        for c in range(1, cols):
            c_copy(k, c).wait_recv()
        for r in range(1, rows):
            d_copy(k, r).wait_recv()
        for side in range(2):
            total = acc[k, side]
            if side == 0:
                for r in range(1, rows):
                    total = total + rec_a[k, r, 0].astype(f32)
                for c in range(1, cols):
                    total = total + fin_a[k, c].astype(f32)
            else:
                for c in range(1, cols):
                    total = total + rec_b[k, c, 0].astype(f32)
                for r in range(1, rows):
                    total = total + fin_b[k, r].astype(f32)
            gate = total[:, :half]
            hbuf[k, at_slot(0, 0), pl.ds(side * half, half)] = (
                gate / (1.0 + jnp.exp(-gate)) * total[:, half:]
            ).astype(bf16)
        for r, c in edges:
            h_copy(k, r, c).start()

    def relay(k):
        for r, c in edges:
            h_copy(k, r, c).wait_recv()
        for r, c in corners:
            relay_a(k, r, c).start()
            relay_b(k, r, c).start()

    down_tile = tile_of(out_cols, 512)

    def emit(k):
        for r, c in corners:
            relay_a(k, r, c).wait_recv()
            relay_b(k, r, c).wait_recv()

        def column(j, _):
            where = pl.ds(pl.multiple_of(j * down_tile, down_tile), down_tile)
            osend[k, :, where] = jnp.dot(hbuf[k], wd[:, where], preferred_element_type=f32).astype(bf16)
            return 0

        lax.fori_loop(0, out_cols // down_tile, column, 0)
        for r, c in others:
            o_copy(k, r, c, (row, col)).start()
        o_own(k).start()

    stages = (project, combine, activate, relay, emit)

    def step(s, _):
        for lag, stage in enumerate(stages):
            k = s - lag

            @pl.when(jnp.logical_and(k >= 0, k < chunks))
            def _():
                stage(k)

            if lag == 0:

                @pl.when(s + AHEAD < chunks)
                def _():
                    send_tokens(s + AHEAD)

                @pl.when(s == 0)
                def _():
                    loads[2].wait()

        return 0

    lax.fori_loop(0, chunks + len(stages) - 1, step, 0)

    def finish(k, _):
        o_own(k).wait()
        for r, c in others:
            x_copy(k, r, c).wait_send()
            o_copy(k, r, c, (row, col)).wait_send()
            o_copy(k, r, c, up(r, c)).wait_recv()
        for r in range(1, rows):
            a_copy(k, r).wait_send()
            d_copy(k, r).wait_send()
        for c in range(1, cols):
            b_copy(k, c).wait_send()
            c_copy(k, c).wait_send()
        for r, c in edges:
            h_copy(k, r, c).wait_send()
        for r, c in corners:
            relay_a(k, r, c).wait_send()
            relay_b(k, r, c).wait_send()
        return 0

    lax.fori_loop(0, chunks, finish, 0)


def solution(mesh):
    rows, cols = mesh.shape["row"], mesh.shape["col"]
    n = rows * cols

    def shards(tokens, w_gate, w_up, w_down):
        count, width = tokens.shape
        features, hidden = w_gate.shape
        out_cols = w_down.shape[1]
        chunks = CHUNKS
        t = count // chunks
        bf16 = jnp.bfloat16
        any_space = pl.BlockSpec(memory_space=pl.ANY)

        def sems(*shape):
            return pltpu.SemaphoreType.DMA((2, chunks, *shape))

        return pl.pallas_call(
            functools.partial(kernel, rows, cols, chunks),
            out_shape=jax.ShapeDtypeStruct((count, width), bf16),
            in_specs=[any_space] * 4,
            out_specs=any_space,
            scratch_shapes=[
                pltpu.VMEM((features, hidden), bf16),
                pltpu.VMEM((features, hidden), bf16),
                pltpu.VMEM((hidden, out_cols), bf16),
                pltpu.VMEM((chunks, n * t, features), bf16),
                pltpu.VMEM((chunks, 2, t, hidden), jnp.float32),
                pltpu.VMEM((chunks, 2, rows, cols, t, hidden), bf16),
                pltpu.VMEM((chunks, rows, cols, t, hidden), bf16),
                pltpu.VMEM((chunks, cols, rows, t, hidden), bf16),
                pltpu.VMEM((chunks, cols, t, hidden), bf16),
                pltpu.VMEM((chunks, rows, t, hidden), bf16),
                pltpu.VMEM((chunks, cols, t, hidden), bf16),
                pltpu.VMEM((chunks, rows, t, hidden), bf16),
                pltpu.VMEM((chunks, n * t, hidden), bf16),
                pltpu.VMEM((chunks, n * t, out_cols), bf16),
                pltpu.SemaphoreType.DMA((3,)),
                sems(n), sems(rows), sems(cols), sems(cols), sems(rows),
                sems(n), sems(n), sems(n), sems(n),
            ],
            compiler_params=pltpu.CompilerParams(collective_id=0, has_side_effects=True),
        )(tokens, w_gate, w_up, w_down)

    in_specs = (
        P(("dp", "row", "col"), None),
        P(("row", "col"), None),
        P(("row", "col"), None),
        P(None, ("row", "col")),
    )
    out_specs = P(("dp", "row", "col"), None)
    return jax.shard_map(shards, mesh=mesh, in_specs=in_specs, out_specs=out_specs, check_vma=False)
```

time: 324 us -> 80.7 us (0.25)
  waiting for transfers between devices: 226 us -> 0 us
  Pallas kernels: 0 us -> 77.5 us
  blocking collectives: 58 us -> 0 us
  matrix products: 16.2 us -> 0 us
  between operations: 13.2 us -> 0.01 us
  local copies, waits for them, and re-layouts: 9.38 us -> 3.1 us
    all_gather x3 -> x0, waiting for transfers between devices: 204 us -> none  [the longest x1 106 us: shards(): lax.all_gather(w_up, 'col', axis=0, tiled=True)]
    pallas_call x0 -> x1, Pallas kernels: none -> 77.5 us  [shards(): pl.pallas_call(functools.partial(kernel, rows, cols, chunks), out_shape=j...]
    all_to_all x2 -> x0, blocking collectives: 58 us -> none  [the longest x1 30.1 us: shards(): lax.all_to_all(tokens, 'row', split_axis=1, concat_axis=0, tiled=True)]
    unnamed x5 -> x0, waiting for transfers between devices: 21.9 us -> none
    dot_general x2 -> x0, matrix products: 16.2 us -> none  [the longest x1 11.3 us: shards(): jnp.dot(col_tokens, paired, preferred_element_type=jnp.float32)]
    all_to_all x2 -> x0, local copies, waits for them, and re-layouts: 4.16 us -> none  [the longest x1 2.71 us: shards(): lax.all_to_all(tokens, 'row', split_axis=1, concat_axis=0, tiled=True)]
  transfers between devices with their start and end apart: 4 -> 0, of which waited for: 4 -> 0; matrix products, arithmetic and copies ran while one was open for 2% -> 0% of each run, Pallas kernels for 0% -> 0%
where the time goes in v2:
time: 80.7 us; the launch traced here: 80.6 us
  Pallas kernels  77.5 us (96%)
  local copies, waits for them, and re-layouts  3.1 us (4%)
    pallas_call x1, Pallas kernels, shards(): pl.pallas_call(functools.partial(kernel, rows, cols, chunks), out_shape=j...  77.5 us
    unnamed x1, local copies, waits for them, and re-layouts  3.1 us

profile of v2, /device:TPU:0, one launch (start us, length us, event | category | flops | bytes accessed | tf_op | source)
XLA Modules:
  0.0 80.6 jit_solution(14043441460151345208)
XLA Ops:
  0.0 77.5 %shard_map.46 = bf16[128,8192]{1,0:T(8,128)(2,1)} custom-call(bf16[128,8192]{1,0:T(8,128)(2,1)} %x_ref.1, bf16[2048,1024]{1,0:T(8,128)(2,1)} %wg_ref.1, bf16[2048,1024]{1,0:T(8,128)(2,1)} %wu_ref.1, bf16[1024,2048]{1,0:T(8,128)(2,1)} %wd_ref.1), custom_call_target="tpu_custom_call" | custom-call | tf_op jit(solution)/shard_map/pallas_call | solution.py:296
  77.5 3.1 %copy.6 = bf16[128,8192]{1,0:T(8,128)(2,1)} copy(bf16[128,8192]{1,0:T(8,128)(2,1)} %shard_map.46) | data formatting | bytes 4194304

commit v3 on v2

--- a/solution.py
+++ b/solution.py
@@ -10,6 +10,7 @@
 MESH = pl.DeviceIdType.MESH
 CHUNKS = 4
 AHEAD = 2
+EARLY_HOPS = 2
 
 
 def tile_of(width, most):
@@ -20,18 +21,23 @@
 
 
 def kernel(
-    rows, cols, chunks,
+    groups, rows, cols, chunks,
     x_ref, wg_ref, wu_ref, wd_ref, out_ref,
-    wg, wu, wd, xbuf, acc, part, rec_a, rec_b, sum_a, sum_b, fin_a, fin_b, hbuf, osend,
-    w_sem, x_sem, a_sem, b_sem, c_sem, d_sem, h_sem, ra_sem, rb_sem, o_sem,
+    wg, wu, wa, wb, xbuf, acc, part, rec_a, rec_b, sum_a, sum_b, fin_a, fin_b, ha, hb, oa, ob,
+    w_sem, fa_sem, fb_sem, up_sem, down_sem, land_sem, mate_sem,
+    x_sem, a_sem, b_sem, c_sem, d_sem, ha_sem, hb_sem, oa_sem, ob_sem,
 ):
     n = rows * cols
     row, col = lax.axis_index("row"), lax.axis_index("col")
-    me = row * cols + col
+    group = lax.axis_index("dp")
+    mates = 2 - groups % 2
+    planes = groups // mates
+    plane, core = group // mates, lax.rem(group, mates)
     t = x_ref.shape[0] // chunks
     features, hidden = wg.shape
     half = hidden // 2
-    out_cols = wd.shape[1]
+    side_cols = wa.shape[2]
+    share = hidden // groups
     bf16, f32 = jnp.bfloat16, jnp.float32
 
     def up(r, c):
@@ -83,48 +89,157 @@
     def d_copy(k, r):
         return remote(sum_b.at[k, r], fin_b.at[k, r], d_sem, (k, r), down(r, 0))
 
-    def h_copy(k, r, c):
+    def share_of(g):
+        return pl.ds(pl.multiple_of(g * share, share), share)
+
+    def fetch_a(c):
         return remote(
-            hbuf.at[k, at_slot(0, 0)], hbuf.at[k, at_slot(r, c)], h_sem, (k, r * cols + c), up(r, c)
-        )
-
-    def relay_a(k, r, c):
+            wd_ref.at[share_of(group), pl.ds(0, side_cols)], wa.at[c, share_of(group)],
+            fa_sem, (c,), down(0, c),
+        )
+
+    def fetch_b(r):
         return remote(
-            hbuf.at[k, at_slot(r, 0), pl.ds(0, half)], hbuf.at[k, at_slot(r, c), pl.ds(0, half)],
-            ra_sem, (k, r * cols + c), up(0, c),
-        )
-
-    def relay_b(k, r, c):
+            wd_ref.at[share_of(group), pl.ds(side_cols, side_cols)], wb.at[r, share_of(group)],
+            fb_sem, (r,), down(r, 0),
+        )
+
+    blocks = [(wa, c, c) for c in range(1, cols)] + [(wb, r, cols + r) for r in range(1, rows)]
+
+    def pass_on(source, block, sems, to_plane):
+        ref, slot, index = block
+        region = ref.at[slot, share_of(source * mates + core)]
+        return pltpu.make_async_remote_copy(
+            src_ref=region, dst_ref=region,
+            send_sem=sems.at[source, index], recv_sem=land_sem.at[source, index],
+            device_id={"dp": to_plane * mates + core}, device_id_type=MESH,
+        )
+
+    def to_mate(source, block, whose):
+        ref, slot, index = block
+        region = ref.at[slot, share_of(source * mates + whose)]
+        return pltpu.make_async_remote_copy(
+            src_ref=region, dst_ref=region,
+            send_sem=mate_sem.at[0, source, index], recv_sem=mate_sem.at[1, source, index],
+            device_id={"dp": plane * mates + (mates - 1 - core)}, device_id_type=MESH,
+        )
+
+    def spread(source, upward, downward):
+        for block in blocks:
+            if mates > 1:
+                to_mate(source, block, core).start()
+            if upward:
+
+                @pl.when(plane + 1 < planes)
+                def _():
+                    pass_on(source, block, up_sem, plane + 1).start()
+
+            if downward:
+
+                @pl.when(plane > 0)
+                def _():
+                    pass_on(source, block, down_sem, plane - 1).start()
+
+    def hop(h):
+        below, above = plane - h, plane + h
+
+        @pl.when(below >= 0)
+        def _():
+            for block in blocks:
+                pass_on(below, block, up_sem, plane).wait_recv()
+            spread(below, True, False)
+
+        @pl.when(above < planes)
+        def _():
+            for block in blocks:
+                pass_on(above, block, down_sem, plane).wait_recv()
+            spread(above, False, True)
+
+    def last_hops():
+        def more(h, _):
+            hop(h)
+            return 0
+
+        lax.fori_loop(EARLY_HOPS + 1, planes, more, 0)
+        if mates > 1:
+
+            def landed(z, _):
+                for block in blocks:
+                    to_mate(z, block, mates - 1 - core).wait_recv()
+                return 0
+
+            lax.fori_loop(0, planes, landed, 0)
+
+    def sent(z, _):
+        for block in blocks:
+            if mates > 1:
+                to_mate(z, block, core).wait_send()
+
+            @pl.when(jnp.logical_and(plane + 1 < planes, z <= plane))
+            def _():
+                pass_on(z, block, up_sem, plane).wait_send()
+
+            @pl.when(jnp.logical_and(plane > 0, z >= plane))
+            def _():
+                pass_on(z, block, down_sem, plane).wait_send()
+
+        return 0
+
+    def ha_copy(k, r):
+        return remote(ha.at[k, pl.ds(0, t)], ha.at[k, pl.ds(r * t, t)], ha_sem, (k, r), up(r, 0))
+
+    def hb_copy(k, c):
+        return remote(hb.at[k, pl.ds(0, t)], hb.at[k, pl.ds(c * t, t)], hb_sem, (k, c), up(0, c))
+
+    def out_at(k, rc, side):
+        start = (rc[0] * cols + rc[1]) * 2 * side_cols + side * side_cols
+        return out_ref.at[tok(k), pl.ds(pl.multiple_of(start, side_cols), side_cols)]
+
+    def oa_copy(k, r, c, columns_of):
         return remote(
-            hbuf.at[k, at_slot(0, c), pl.ds(half, half)], hbuf.at[k, at_slot(r, c), pl.ds(half, half)],
-            rb_sem, (k, r * cols + c), up(r, 0),
-        )
-
-    def o_copy(k, r, c, columns_of):
+            oa.at[k, c, pl.ds(r * t, t)], out_at(k, columns_of, 0), oa_sem, (k, r, c), down(r, 0)
+        )
+
+    def ob_copy(k, r, c, columns_of):
         return remote(
-            osend.at[k, at_slot(r, c)], out_ref.at[tok(k), shard(columns_of, out_cols)],
-            o_sem, (k, r * cols + c), down(r, c),
-        )
-
-    def o_own(k):
+            ob.at[k, r, pl.ds(c * t, t)], out_at(k, columns_of, 1), ob_sem, (k, r, c), down(0, c)
+        )
+
+    def oa_own(k, c):
         return pltpu.make_async_copy(
-            osend.at[k, at_slot(0, 0)], out_ref.at[tok(k), shard((row, col), out_cols)], o_sem.at[1, k, 0]
-        )
-
-    edges = [(r, c) for r, c in others if r == 0 or c == 0]
-    corners = [(r, c) for r, c in others if r and c]
+            oa.at[k, c, pl.ds(0, t)], out_at(k, up(0, c), 0), oa_sem.at[1, k, 0, c]
+        )
+
+    def ob_own(k, r):
+        return pltpu.make_async_copy(
+            ob.at[k, r, pl.ds(0, t)], out_at(k, up(r, 0), 1), ob_sem.at[1, k, r, 0]
+        )
 
     loads = [
         pltpu.make_async_copy(wg_ref, wg, w_sem.at[0]),
         pltpu.make_async_copy(wu_ref, wu, w_sem.at[1]),
-        pltpu.make_async_copy(wd_ref, wd, w_sem.at[2]),
+        pltpu.make_async_copy(wd_ref.at[:, pl.ds(0, side_cols)], wa.at[0], w_sem.at[2]),
+        pltpu.make_async_copy(wd_ref.at[:, pl.ds(side_cols, side_cols)], wb.at[0], w_sem.at[3]),
     ]
 
     barrier = pltpu.get_barrier_semaphore()
     for r, c in others:
         to = up(r, c)
         pl.semaphore_signal(barrier, inc=1, device_id={"row": to[0], "col": to[1]}, device_id_type=MESH)
-    pl.semaphore_wait(barrier, n - 1)
+    def greet(g):
+        pl.semaphore_signal(barrier, inc=1, device_id={"dp": g}, device_id_type=MESH)
+
+    pl.when(plane > 0)(lambda: greet(group - mates))
+    pl.when(plane + 1 < planes)(lambda: greet(group + mates))
+    if mates > 1:
+        greet(plane * mates + (mates - 1 - core))
+    neighbours = (plane > 0).astype(jnp.int32) + (plane + 1 < planes).astype(jnp.int32)
+    pl.semaphore_wait(barrier, n - 1 + mates - 1 + neighbours)
+
+    for c in range(1, cols):
+        fetch_a(c).start()
+    for r in range(1, rows):
+        fetch_b(r).start()
 
     def send_tokens(k):
         for r, c in others:
@@ -136,8 +251,13 @@
         x_own(k).start()
     for load in loads:
         load.start()
-    loads[0].wait()
-    loads[1].wait()
+    for c in range(1, cols):
+        fetch_a(c).wait_recv()
+    for r in range(1, rows):
+        fetch_b(r).wait_recv()
+    spread(plane, True, True)
+    for load in loads:
+        load.wait()
 
     tile = tile_of(half, 512)
     per_half = half // tile
@@ -201,37 +321,54 @@
                 for r in range(1, rows):
                     total = total + fin_b[k, r].astype(f32)
             gate = total[:, :half]
-            hbuf[k, at_slot(0, 0), pl.ds(side * half, half)] = (
-                gate / (1.0 + jnp.exp(-gate)) * total[:, half:]
+            done = (gate / (1.0 + jnp.exp(-gate)) * total[:, half:]).astype(bf16)
+            ha[k, pl.ds(0, t), pl.ds(side * half, half)] = done
+            hb[k, pl.ds(0, t), pl.ds(side * half, half)] = done
+        for r in range(1, rows):
+            ha_copy(k, r).start()
+        for c in range(1, cols):
+            hb_copy(k, c).start()
+
+    out_tile = tile_of(side_cols, 512)
+    out_tiles = side_cols // out_tile
+
+    def emit(k):
+        for r in range(1, rows):
+            ha_copy(k, r).wait_recv()
+
+        def columns_a(j, _):
+            c = j // out_tiles
+            where = pl.ds(pl.multiple_of(lax.rem(j, out_tiles) * out_tile, out_tile), out_tile)
+            oa[k, c, :, where] = jnp.dot(
+                ha[k], wa[c, :, where], preferred_element_type=f32
             ).astype(bf16)
-        for r, c in edges:
-            h_copy(k, r, c).start()
-
-    def relay(k):
-        for r, c in edges:
-            h_copy(k, r, c).wait_recv()
-        for r, c in corners:
-            relay_a(k, r, c).start()
-            relay_b(k, r, c).start()
-
-    down_tile = tile_of(out_cols, 512)
-
-    def emit(k):
-        for r, c in corners:
-            relay_a(k, r, c).wait_recv()
-            relay_b(k, r, c).wait_recv()
-
-        def column(j, _):
-            where = pl.ds(pl.multiple_of(j * down_tile, down_tile), down_tile)
-            osend[k, :, where] = jnp.dot(hbuf[k], wd[:, where], preferred_element_type=f32).astype(bf16)
             return 0
 
-        lax.fori_loop(0, out_cols // down_tile, column, 0)
-        for r, c in others:
-            o_copy(k, r, c, (row, col)).start()
-        o_own(k).start()
-
-    stages = (project, combine, activate, relay, emit)
+        lax.fori_loop(0, cols * out_tiles, columns_a, 0)
+        for c in range(cols):
+            for r in range(1, rows):
+                oa_copy(k, r, c, up(0, c)).start()
+        for c in range(1, cols):
+            hb_copy(k, c).wait_recv()
+
+        def columns_b(j, _):
+            r = j // out_tiles
+            where = pl.ds(pl.multiple_of(lax.rem(j, out_tiles) * out_tile, out_tile), out_tile)
+            ob[k, r, :, where] = jnp.dot(
+                hb[k], wb[r, :, where], preferred_element_type=f32
+            ).astype(bf16)
+            return 0
+
+        lax.fori_loop(0, rows * out_tiles, columns_b, 0)
+        for r in range(rows):
+            for c in range(1, cols):
+                ob_copy(k, r, c, up(r, 0)).start()
+        for c in range(cols):
+            oa_own(k, c).start()
+        for r in range(rows):
+            ob_own(k, r).start()
+
+    stages = (project, combine, activate, emit)
 
     def step(s, _):
         for lag, stage in enumerate(stages):
@@ -247,44 +384,56 @@
                 def _():
                     send_tokens(s + AHEAD)
 
-                @pl.when(s == 0)
-                def _():
-                    loads[2].wait()
+                for h in range(1, min(EARLY_HOPS, planes - 1) + 1):
+                    pl.when(s == h)(lambda h=h: hop(h))
+
+                pl.when(s == len(stages) - 1)(last_hops)
 
         return 0
 
     lax.fori_loop(0, chunks + len(stages) - 1, step, 0)
 
     def finish(k, _):
-        o_own(k).wait()
         for r, c in others:
             x_copy(k, r, c).wait_send()
-            o_copy(k, r, c, (row, col)).wait_send()
-            o_copy(k, r, c, up(r, c)).wait_recv()
+        for r, c in slots:
+            if r:
+                oa_copy(k, r, c, up(0, c)).wait_send()
+                oa_copy(k, r, c, up(r, c)).wait_recv()
+            else:
+                oa_own(k, c).wait()
+            if c:
+                ob_copy(k, r, c, up(r, 0)).wait_send()
+                ob_copy(k, r, c, up(r, c)).wait_recv()
+            else:
+                ob_own(k, r).wait()
         for r in range(1, rows):
             a_copy(k, r).wait_send()
             d_copy(k, r).wait_send()
+            ha_copy(k, r).wait_send()
         for c in range(1, cols):
             b_copy(k, c).wait_send()
             c_copy(k, c).wait_send()
-        for r, c in edges:
-            h_copy(k, r, c).wait_send()
-        for r, c in corners:
-            relay_a(k, r, c).wait_send()
-            relay_b(k, r, c).wait_send()
+            hb_copy(k, c).wait_send()
         return 0
 
     lax.fori_loop(0, chunks, finish, 0)
+    for c in range(1, cols):
+        fetch_a(c).wait_send()
+    for r in range(1, rows):
+        fetch_b(r).wait_send()
+    lax.fori_loop(0, planes, sent, 0)
 
 
 def solution(mesh):
-    rows, cols = mesh.shape["row"], mesh.shape["col"]
+    groups, rows, cols = mesh.shape["dp"], mesh.shape["row"], mesh.shape["col"]
+    planes = groups // (2 - groups % 2)
     n = rows * cols
 
     def shards(tokens, w_gate, w_up, w_down):
         count, width = tokens.shape
         features, hidden = w_gate.shape
-        out_cols = w_down.shape[1]
+        side_cols = w_down.shape[1] // 2
         chunks = CHUNKS
         t = count // chunks
         bf16 = jnp.bfloat16
@@ -294,14 +443,15 @@
             return pltpu.SemaphoreType.DMA((2, chunks, *shape))
 
         return pl.pallas_call(
-            functools.partial(kernel, rows, cols, chunks),
+            functools.partial(kernel, groups, rows, cols, chunks),
             out_shape=jax.ShapeDtypeStruct((count, width), bf16),
             in_specs=[any_space] * 4,
             out_specs=any_space,
             scratch_shapes=[
                 pltpu.VMEM((features, hidden), bf16),
                 pltpu.VMEM((features, hidden), bf16),
-                pltpu.VMEM((hidden, out_cols), bf16),
+                pltpu.VMEM((cols, hidden, side_cols), bf16),
+                pltpu.VMEM((rows, hidden, side_cols), bf16),
                 pltpu.VMEM((chunks, n * t, features), bf16),
                 pltpu.VMEM((chunks, 2, t, hidden), jnp.float32),
                 pltpu.VMEM((chunks, 2, rows, cols, t, hidden), bf16),
@@ -311,11 +461,19 @@
                 pltpu.VMEM((chunks, rows, t, hidden), bf16),
                 pltpu.VMEM((chunks, cols, t, hidden), bf16),
                 pltpu.VMEM((chunks, rows, t, hidden), bf16),
-                pltpu.VMEM((chunks, n * t, hidden), bf16),
-                pltpu.VMEM((chunks, n * t, out_cols), bf16),
-                pltpu.SemaphoreType.DMA((3,)),
+                pltpu.VMEM((chunks, rows * t, hidden), bf16),
+                pltpu.VMEM((chunks, cols * t, hidden), bf16),
+                pltpu.VMEM((chunks, cols, rows * t, side_cols), bf16),
+                pltpu.VMEM((chunks, rows, cols * t, side_cols), bf16),
+                pltpu.SemaphoreType.DMA((4,)),
+                pltpu.SemaphoreType.DMA((2, cols)),
+                pltpu.SemaphoreType.DMA((2, rows)),
+                pltpu.SemaphoreType.DMA((planes, cols + rows)),
+                pltpu.SemaphoreType.DMA((planes, cols + rows)),
+                pltpu.SemaphoreType.DMA((planes, cols + rows)),
+                pltpu.SemaphoreType.DMA((2, planes, cols + rows)),
                 sems(n), sems(rows), sems(cols), sems(cols), sems(rows),
-                sems(n), sems(n), sems(n), sems(n),
+                sems(rows), sems(cols), sems(rows, cols), sems(rows, cols),
             ],
             compiler_params=pltpu.CompilerParams(collective_id=0, has_side_effects=True),
         )(tokens, w_gate, w_up, w_down)

time: 80.7 us -> 76 us (0.942); the launches traced: 80.6 us -> 74.5 us
  Pallas kernels: 77.5 us -> 71.4 us
    pallas_call x1, Pallas kernels: 77.5 us -> 71.4 us  [shards(): pl.pallas_call(functools.partial(kernel, groups, rows, cols, chunks), out...]
where the time goes in v3:
time: 76 us; the launch traced here: 74.5 us
  Pallas kernels  71.4 us (94%)
  local copies, waits for them, and re-layouts  3.1 us (4%)
    pallas_call x1, Pallas kernels, shards(): pl.pallas_call(functools.partial(kernel, groups, rows, cols, chunks), out...  71.4 us
    unnamed x1, local copies, waits for them, and re-layouts  3.1 us

profile of v3, /device:TPU:0, one launch (start us, length us, event | category | flops | bytes accessed | tf_op | source)
XLA Modules:
  0.0 74.5 jit_solution(4723577324404666170)
XLA Ops:
  0.0 71.4 %shard_map.46 = bf16[128,8192]{1,0:T(8,128)(2,1)} custom-call(bf16[128,8192]{1,0:T(8,128)(2,1)} %x_ref.1, bf16[2048,1024]{1,0:T(8,128)(2,1)} %wg_ref.1, bf16[2048,1024]{1,0:T(8,128)(2,1)} %wu_ref.1, bf16[1024,2048]{1,0:T(8,128)(2,1)} %wd_ref.1), custom_call_target="tpu_custom_call" | custom-call | tf_op jit(solution)/shard_map/pallas_call | solution.py:445
  71.5 3.1 %copy.6 = bf16[128,8192]{1,0:T(8,128)(2,1)} copy(bf16[128,8192]{1,0:T(8,128)(2,1)} %shard_map.46) | data formatting | bytes 4194304

commit v4 on v3

--- a/solution.py
+++ b/solution.py
@@ -9,7 +9,7 @@
 
 MESH = pl.DeviceIdType.MESH
 CHUNKS = 4
-AHEAD = 2
+AHEAD = 3
 EARLY_HOPS = 2
 
 
@@ -61,6 +61,7 @@
 
     slots = [(r, c) for r in range(rows) for c in range(cols)]
     others = slots[1:]
+    by_reach = others[::-1]
 
     def at_slot(r, c):
         return pl.ds((r * cols + c) * t, t)
@@ -242,7 +243,7 @@
         fetch_b(r).start()
 
     def send_tokens(k):
-        for r, c in others:
+        for r, c in by_reach:
             x_copy(k, r, c).start()
 
     for k in range(min(AHEAD, chunks)):

time: 76 us -> 75.1 us (0.988)
  Pallas kernels: 71.4 us -> 70.6 us
    pallas_call x1, Pallas kernels: 71.4 us -> 70.6 us  [shards(): pl.pallas_call(functools.partial(kernel, groups, rows, cols, chunks), out...]
where the time goes in v4:
time: 75.1 us; the launch traced here: 73.7 us
  Pallas kernels  70.6 us (94%)
  local copies, waits for them, and re-layouts  3.1 us (4%)
    pallas_call x1, Pallas kernels, shards(): pl.pallas_call(functools.partial(kernel, groups, rows, cols, chunks), out...  70.6 us
    unnamed x1, local copies, waits for them, and re-layouts  3.1 us

profile of v4, /device:TPU:0, one launch (start us, length us, event | category | flops | bytes accessed | tf_op | source)
XLA Modules:
  0.0 73.7 jit_solution(14746550104305296161)
XLA Ops:
  0.0 70.6 %shard_map.46 = bf16[128,8192]{1,0:T(8,128)(2,1)} custom-call(bf16[128,8192]{1,0:T(8,128)(2,1)} %x_ref.1, bf16[2048,1024]{1,0:T(8,128)(2,1)} %wg_ref.1, bf16[2048,1024]{1,0:T(8,128)(2,1)} %wu_ref.1, bf16[1024,2048]{1,0:T(8,128)(2,1)} %wd_ref.1), custom_call_target="tpu_custom_call" | custom-call | tf_op jit(solution)/shard_map/pallas_call | solution.py:446
  70.6 3.1 %copy.6 = bf16[128,8192]{1,0:T(8,128)(2,1)} copy(bf16[128,8192]{1,0:T(8,128)(2,1)} %shard_map.46) | data formatting | bytes 4194304
